TPU v7x, 32 devices: a whole 2x2x4 slice. The times are simulated.
32 devices in a mesh: sub: 2 (over y), row: 4 (over x, core), col: 4 (over z).
Axes of the slice: x: 2, y: 2, z: 4, core: 2. Of those that a mesh axis runs over, the one named last changes fastest.
Arguments:
- factor_window: bfloat16 [2, 8192, 1024], P('sub', ('row', 'col'))
- right_sides: bfloat16 [2, 8192, 2048], P('sub', 'row', 'col'), may hold values from -1.1953125 to 1.1953125
- first_block: int32 [2, 8], P('sub'), may hold values from 0 to 4
- tile_map: int32 [2, 8], P('sub'), may hold values from 0 to 15, as said below
- interface_block: float32 [4096, 4096], P(('sub', 'row'), 'col'), may hold values from -6 to 6
Outputs:
- updated_sides: bfloat16 [2, 8192, 2048], P('sub', 'row', 'col')
- schur_global: float32 [4096, 4096], P(('sub', 'row'), 'col')
Inputs may be any that keep to these rules, and one draw needn't show every extreme that they name: `tile_map`: the 8 entries of a subdomain are different global tiles.
All inputs are finite; a program needn't handle non-finite values.
Results may differ from a plain program's by a relative error of at most 0.0075.
Values may be sent and summed in bfloat16 or wider, within the bound.
A program may use at most 64 MiB of HBM per device.

v0:
```python
import jax
import jax.numpy as jnp
from jax import lax
from jax.sharding import PartitionSpec as P

PANEL = 256
BLOCK = 256
STEPS = 4
GTILES = 16


def spread_2(value, axis, source):
    kept = jnp.where(lax.axis_index(axis) == source, value, 0).astype(value.dtype)
    return lax.psum(kept, axis)


def spread_tiles(columns, tile_map, block_count):
    onehot = (tile_map[0][:, None] == jnp.arange(GTILES, dtype=jnp.int32)[None, :]).astype(
        jnp.bfloat16
    )
    height = columns.shape[0]
    spread = jnp.einsum(
        "qbj,bg->qgj",
        columns.reshape(height, block_count, BLOCK),
        onehot,
        preferred_element_type=jnp.float32,
    )
    return spread.reshape(height, GTILES * BLOCK).astype(jnp.bfloat16)


def local(factor_window, right_sides, first_block, tile_map, interface_block):
    row_count = lax.axis_size("row")
    row_pos = lax.axis_index("row")
    col_pos = lax.axis_index("col")
    local_factor = factor_window[0]
    local_sides = right_sides[0]
    block_rows = local_sides.shape[0]
    block_cols = local_sides.shape[1]
    block_count = first_block.shape[1]
    row_global = row_pos * block_rows + jnp.arange(block_rows, dtype=jnp.int32)
    col_global = col_pos * block_cols + jnp.arange(block_cols, dtype=jnp.int32)
    col_block = col_global // BLOCK
    block_ids = jnp.arange(block_count, dtype=jnp.int32)
    first_col = jnp.sum(
        jnp.where(col_block[:, None] == block_ids[None, :], first_block[0][None, :], 0), axis=1
    )
    live = (row_global // PANEL)[:, None] >= first_col[None, :]
    current = jnp.where(live, local_sides.astype(jnp.float32), jnp.float32(0.0))
    is_root = row_pos == 0
    factor_rows = lax.all_gather(local_factor, "col", axis=0, tiled=True)
    pieces = []
    for panel in range(STEPS):
        offset = panel * PANEL
        panel_cols = factor_rows[:, offset : offset + PANEL]
        diag_block = panel_cols[offset : offset + PANEL].astype(jnp.float32)
        diag_block = jnp.where(is_root, diag_block, jnp.eye(PANEL, dtype=jnp.float32))
        solved = jax.scipy.linalg.solve_triangular(
            diag_block, current[offset : offset + PANEL], lower=True
        ).astype(jnp.bfloat16)
        solved = spread_2(solved, "row", 0)
        update = jnp.dot(panel_cols, solved, preferred_element_type=jnp.float32)
        current = jnp.where((row_global >= offset + PANEL)[:, None], current - update, current)
        placed = jnp.where(is_root, solved.astype(jnp.float32), current[offset : offset + PANEL])
        current = current.at[offset : offset + PANEL].set(placed)
        pieces.append(solved)
    updated_sides = current.astype(jnp.bfloat16)[None]
    stacked = jnp.concatenate(pieces, axis=0)
    out_cols = interface_block.shape[1]
    share = stacked.shape[0] // row_count
    my_share = lax.dynamic_slice_in_dim(stacked, row_pos * share, share, 0)
    all_columns = lax.all_gather(my_share, "col", axis=1, tiled=True)
    spread = spread_tiles(all_columns, tile_map, block_count)
    my_columns = lax.dynamic_slice_in_dim(spread, col_pos * out_cols, out_cols, 1)
    summed = lax.psum_scatter(
        lax.dot_general(
            spread, my_columns, (((0,), (0,)), ((), ())), preferred_element_type=jnp.float32
        ).astype(jnp.bfloat16),
        ("sub", "row"),
        scatter_dimension=0,
        tiled=True,
    ).astype(jnp.float32)
    schur_global = interface_block - summed
    return (updated_sides, schur_global)


def solution(mesh):
    return jax.shard_map(
        local,
        mesh=mesh,
        in_specs=(
            P("sub", ("row", "col"), None),
            P("sub", "row", "col"),
            P("sub", None),
            P("sub", None),
            P(("sub", "row"), "col"),
        ),
        out_specs=(P("sub", "row", "col"), P(("sub", "row"), "col")),
        check_vma=False,
    )
```

profile of v0, /device:TPU:0, one launch (start us, length us, event | category | flops | bytes accessed | tf_op | source)
XLA Modules:
  0.0 394.8 jit_solution(10873900418680429173)
XLA Ops:
  7.2 0.7 all-gather.6.cloned.1.call-update
  8.0 0.7 select_reduce_fusion
  8.8 3.5 convert_select_fusion
  12.3 80.8 %all-gather.6.cloned.1.call-done = bf16[1,2048,1024]{2,1,0:T(8,128)(2,1)} async-done(((bf16[1,512,1024]{2,1,0:T(8,128)(2,1)}), bf16[1,2048,1024]{2,1,0:T(8,128)(2,1)}) %all-gather.6.cloned.1.call-update) | async-done | bytes 4194320 | tf_op jit(solution)/shard_map/all_gather | solution.py:50
  93.0 1.2 fusion.16
  94.3 3.8 while.12
  94.9 1.3 bitcast_dynamic-update-slice_fusion.8
  96.8 1.3 bitcast_dynamic-update-slice_fusion.8
  98.1 19.7 %custom-call.6 = f32[2,128,128]{1,2,0:T(8,128)S(1)} custom-call(f32[2,128,128]{2,1,0:T(8,128)S(1)} %get-tuple-element.77), custom_call_target="InvertDiagBlocksLowerTriangular" | custom-call | tf_op jit(solution)/shard_map/jit(_solve_triangular)/triangular_solve | solution.py:57
  117.8 1.4 fusion.26
  119.2 1.3 convolution_subtract_fusion.3
  120.9 0.7 fusion.12
  121.7 4.0 %while.13 = (s32[]{:T(128)}, f32[256,256]{1,0:T(8,128)S(1)}, s32[2,2]{1,0:T(2,128)S(1)}, f32[2,128,128]{2,1,0:T(8,128)S(1)}, s32[]{:T(128)}) while((s32[]{:T(128)}, f32[256,256]{1,0:T(8,128)S(1)}, s32[2,2]{1,0:T(2,128)S(1)}, f32[2,128,128]{2,1,0:T(8,128)S(1)}, s32[]{:T(128)}) %tuple.113), condition=%wide.while_cond.4.clone, body=%wide.while_body.4.clone.sunk | while | flops 2 | bytes 131181 | solution.py:57
  121.8 0.7 fusion.73
  122.4 1.3 bitcast_dynamic-update-slice_fusion.9
  123.8 0.7 fusion.73
  124.5 1.3 bitcast_dynamic-update-slice_fusion.9
  125.8 19.7 %custom-call.7 = f32[2,128,128]{1,2,0:T(8,128)S(1)} custom-call(f32[2,128,128]{2,1,0:T(8,128)S(1)} %get-tuple-element.78), custom_call_target="InvertDiagBlocksLowerTriangular" | custom-call | tf_op jit(solution)/shard_map/jit(_solve_triangular)/triangular_solve | solution.py:57
  145.5 7.4 %all-reduce.5.cloned.1.call-done = bf16[256,512]{1,0:T(8,128)(2,1)} async-done(((bf16[256,512]{1,0:T(8,128)(2,1)}), bf16[256,512]{1,0:T(8,128)(2,1)}) %all-reduce.5.cloned.1.call-update) | async-done | bytes 262160 | tf_op jit(solution)/shard_map/psum | solution.py:14
  152.9 3.4 subtract_select_fusion.3
  156.8 1.6 copy-done.2
  159.2 0.7 fusion.11
  160.2 4.0 %while.14 = (s32[]{:T(128)}, f32[256,256]{1,0:T(8,128)S(1)}, s32[2,2]{1,0:T(2,128)S(1)}, f32[2,128,128]{2,1,0:T(8,128)S(1)}, s32[]{:T(128)}) while((s32[]{:T(128)}, f32[256,256]{1,0:T(8,128)S(1)}, s32[2,2]{1,0:T(2,128)S(1)}, f32[2,128,128]{2,1,0:T(8,128)S(1)}, s32[]{:T(128)}) %tuple.114), condition=%wide.while_cond.4.clone.1, body=%wide.while_body.4.clone.1.sunk | while | flops 2 | bytes 131181 | solution.py:57
  160.8 1.4 bitcast_dynamic-update-slice_fusion.10
  162.8 1.4 bitcast_dynamic-update-slice_fusion.10
  164.2 19.7 %custom-call.8 = f32[2,128,128]{1,2,0:T(8,128)S(1)} custom-call(f32[2,128,128]{2,1,0:T(8,128)S(1)} %get-tuple-element.79), custom_call_target="InvertDiagBlocksLowerTriangular" | custom-call | tf_op jit(solution)/shard_map/jit(_solve_triangular)/triangular_solve | solution.py:57
  183.9 8.8 %all-reduce.7.cloned.1.call-done = bf16[256,512]{1,0:T(8,128)(2,1)} async-done(((bf16[256,512]{1,0:T(8,128)(2,1)}), bf16[256,512]{1,0:T(8,128)(2,1)}) %all-reduce.7.cloned.1.call-update) | async-done | bytes 262160 | tf_op jit(solution)/shard_map/psum | solution.py:14
  192.7 3.4 subtract_select_fusion.2
  196.7 1.6 copy-done.1
  199.0 0.7 fusion.10
  199.9 3.8 while.15
  200.5 1.3 bitcast_dynamic-update-slice_fusion.11
  202.4 1.3 bitcast_dynamic-update-slice_fusion.11
  203.7 19.7 %custom-call.9 = f32[2,128,128]{1,2,0:T(8,128)S(1)} custom-call(f32[2,128,128]{2,1,0:T(8,128)S(1)} %get-tuple-element.80), custom_call_target="InvertDiagBlocksLowerTriangular" | custom-call | tf_op jit(solution)/shard_map/jit(_solve_triangular)/triangular_solve | solution.py:57
  223.4 9.2 %all-reduce.9.cloned.1.call-done = bf16[256,512]{1,0:T(8,128)(2,1)} async-done(((bf16[256,512]{1,0:T(8,128)(2,1)}), bf16[256,512]{1,0:T(8,128)(2,1)}) %all-reduce.9.cloned.1.call-update) | async-done | bytes 262160 | tf_op jit(solution)/shard_map/psum | solution.py:14
  232.5 3.4 subtract_select_fusion.1
  236.5 1.6 copy-done
  238.8 0.7 fusion.9
  239.7 32.3 %all-reduce.11.cloned.1.call-done = bf16[256,512]{1,0:T(8,128)(2,1)} async-done(((bf16[256,512]{1,0:T(8,128)(2,1)}), bf16[256,512]{1,0:T(8,128)(2,1)}) %all-reduce.11.cloned.1.call-update) | async-done | bytes 262160 | tf_op jit(solution)/shard_map/psum | solution.py:14
  272.0 3.4 subtract_select_fusion
  275.4 1.6 fusion.19
  277.2 27.9 %all-gather.4.cloned.1.call-done = bf16[256,2048]{1,0:T(8,128)(2,1)} async-done(((bf16[256,512]{1,0:T(8,128)(2,1)}), bf16[256,2048]{1,0:T(8,128)(2,1)}) %all-gather.4.cloned.1.call-update) | async-done | bytes 1048592 | tf_op jit(solution)/shard_map/all_gather | solution.py:71
  305.1 1.5 copy.19
  306.7 0.8 convolution_convert_fusion.1
  307.5 0.9 copy.20
  308.4 5.6 %convolution_convert_fusion = bf16[4096,1024]{1,0:T(8,128)(2,1)} fusion(bf16[256,4096]{1,0:T(8,128)(2,1)S(1)} %bitcast.105, s32[]{:T(128)S(6)} %select_n.126), kind=kOutput, calls=%fused_computation.8 | convolution fusion | flops 2151677952 | bytes 11010052 | tf_op jit(solution)/shard_map/dot_general | solution.py:75
  314.1 71.0 %reduce-scatter.2.cloned.1.call-done = bf16[512,1024]{1,0:T(8,128)(2,1)} async-done(((bf16[4096,1024]{1,0:T(8,128)(2,1)}), bf16[512,1024]{1,0:T(8,128)(2,1)}) %reduce-scatter.2.cloned.1.call-update) | async-done | bytes 1048592 | tf_op jit(solution)/shard_map/reduce_scatter | solution.py:74
  385.1 2.8 convert_subtract_fusion
  (71 shorter events, 9.0 us)
Async XLA Ops:
  7.2 85.9 %all-gather.6.cloned.1.call-start = ((), (), s32[]{:S(2)}) async-start(), calls=%async_computation.7 | async-start | bytes 5242880 | tf_op jit(solution)/shard_map/all_gather | solution.py:50
  7.9 145.0 %all-reduce.5.cloned.1.call-start = ((), (), s32[]{:S(2)}) async-start(), calls=%async_computation.1 | async-start | bytes 524288 | tf_op jit(solution)/shard_map/psum | solution.py:14
  12.3 140.6 %copy-start.6 = (bf16[1,2048,512]{2,1,0:T(8,128)(2,1)S(1)}, bf16[1,2048,512]{2,1,0:T(8,128)(2,1)}, u32[]{:S(2)}) copy-start(bf16[1,2048,512]{2,1,0:T(8,128)(2,1)} %param.16) | copy-start | bytes 6291460
  121.7 71.0 %all-reduce.7.cloned.1.call-start = ((), (), s32[]{:S(2)}) async-start(), calls=%async_computation.2 | async-start | bytes 524288 | tf_op jit(solution)/shard_map/psum | solution.py:14
  152.9 3.4 copy-start.8
  156.4 2.0 copy-start.2
  160.0 72.6 %all-reduce.9.cloned.1.call-start = ((), (), s32[]{:S(2)}) async-start(), calls=%async_computation.3 | async-start | bytes 524288 | tf_op jit(solution)/shard_map/psum | solution.py:14
  192.7 3.4 copy-start.4
  196.2 2.0 copy-start.1
  199.8 72.2 %all-reduce.11.cloned.1.call-start = ((), (), s32[]{:S(2)}) async-start(), calls=%async_computation.4 | async-start | bytes 524288 | tf_op jit(solution)/shard_map/psum | solution.py:14
  232.5 3.4 copy-start.5
  236.0 2.0 copy-start
  239.6 65.5 %all-gather.4.cloned.1.call-start = ((), (), s32[]{:S(2)}) async-start(), calls=%async_computation.5 | async-start | bytes 1310720 | tf_op jit(solution)/shard_map/all_gather | solution.py:71
  239.7 67.0 %copy-start.10 = (s32[1,8]{1,0:T(1,128)S(1)}, s32[1,8]{1,0:T(1,128)}, u32[]{:S(2)}) copy-start(s32[1,8]{1,0:T(1,128)} %param.18) | copy-start | bytes 100
  272.0 3.4 copy-start.9
  276.9 31.5 %copy-start.3 = (bf16[2048,512]{1,0:T(8,128)(2,1)}, bf16[2048,512]{1,0:T(8,128)(2,1)S(1)}, u32[]{:S(2)}) copy-start(bf16[2048,512]{1,0:T(8,128)(2,1)S(1)} %get-tuple-element.126) | copy-start | bytes 6291460
  277.0 108.2 %reduce-scatter.2.cloned.1.call-start = ((), (), s32[]{:S(2)}) async-start(), calls=%async_computation.6 | async-start | bytes 9437184 | tf_op jit(solution)/shard_map/reduce_scatter | solution.py:74
  314.1 71.1 %copy-start.7 = (f32[512,1024]{1,0:T(8,128)S(1)}, f32[512,1024]{1,0:T(8,128)}, u32[]{:S(2)}) copy-start(f32[512,1024]{1,0:T(8,128)} %param.19) | copy-start | bytes 6291460
Sparse Core Ops, SparseCore 0:
  9.5 83.4 all-gather.5
  121.8 31.0 all-reduce.4
  160.1 32.5 all-reduce.6
  199.9 32.5 all-reduce.8
  239.7 32.2 all-reduce.10
  277.1 27.9 all-gather.3
  314.2 70.8 reduce-scatter.1
where the time goes:
time: 395 us
  waiting for transfers between devices  238 us (60%)
  other arithmetic  92 us (23%)
  matrix products  26.7 us (7%)
  local copies, waits for them, and re-layouts  22.7 us (6%)
  between operations  14.5 us (4%)
    all_gather x1, waiting for transfers between devices, local(): factor_rows = lax.all_gather(local_factor, 'col', axis=0, tiled=True)  80.8 us
    another operation x6, other arithmetic, local(): jax.scipy.linalg.solve_triangular(diag_block, current[offset:offset + PAN...  79.9 us
    reduce_scatter x1, waiting for transfers between devices, local(): lax.psum_scatter(lax.dot_general(spread, my_columns, (((0,), (0,)), ((),...  71 us
    psum x4, waiting for transfers between devices, spread_2(): return lax.psum(kept, axis)  57.7 us
    all_gather x1, waiting for transfers between devices, local(): all_columns = lax.all_gather(my_share, 'col', axis=1, tiled=True)  27.9 us
    another operation x29, local copies, waits for them, and re-layouts, local(): jax.scipy.linalg.solve_triangular(diag_block, current[offset:offset + PAN...  15.5 us
    dot_general x4, matrix products, local(): update = jnp.dot(panel_cols, solved, preferred_element_type=jnp.float32)  13.4 us
  transfers between devices with their start and end apart: 7, of which 7 were waited for; matrix products, arithmetic and copies ran while one was open for 19% of the time, Pallas kernels for 0%

commit v1 on v0

--- a/solution.py
+++ b/solution.py
@@ -11,7 +11,7 @@
 
 def spread_2(value, axis, source):
     kept = jnp.where(lax.axis_index(axis) == source, value, 0).astype(value.dtype)
-    return lax.psum(kept, axis)
+    return jnp.sum(lax.all_gather(kept, axis), axis=0)
 
 
 def spread_tiles(columns, tile_map, block_count):

time: 395 us -> 358 us (0.906)
  waiting for transfers between devices: 238 us -> 196 us
  other arithmetic: 92 us -> 97.8 us
    psum x4 -> x0, waiting for transfers between devices: 57.7 us -> none  [spread_2(): return lax.psum(kept, axis)]
    all_gather x0 -> x4, waiting for transfers between devices: none -> 15.4 us  [spread_2(): return jnp.sum(lax.all_gather(kept, axis), axis=0)]
    reduce_sum x0 -> x4, other arithmetic: none -> 5.82 us  [spread_2(): return jnp.sum(lax.all_gather(kept, axis), axis=0)]
  transfers between devices with their start and end apart: 7 -> 7, of which waited for: 7 -> 4; matrix products, arithmetic and copies ran while one was open for 19% -> 21% of each run, Pallas kernels for 0% -> 0%
where the time goes in v1:
time: 358 us
  waiting for transfers between devices  196 us (55%)
  other arithmetic  97.8 us (27%)
  matrix products  26.2 us (7%)
  local copies, waits for them, and re-layouts  22.3 us (6%)
  between operations  14.5 us (4%)
    all_gather x1, waiting for transfers between devices, local(): factor_rows = lax.all_gather(local_factor, 'col', axis=0, tiled=True)  80.8 us
    another operation x6, other arithmetic, local(): jax.scipy.linalg.solve_triangular(diag_block, current[offset:offset + PAN...  79.9 us
    reduce_scatter x1, waiting for transfers between devices, local(): lax.psum_scatter(lax.dot_general(spread, my_columns, (((0,), (0,)), ((),...  71 us
    all_gather x1, waiting for transfers between devices, local(): all_columns = lax.all_gather(my_share, 'col', axis=1, tiled=True)  27.9 us
    all_gather x4, waiting for transfers between devices, spread_2(): return jnp.sum(lax.all_gather(kept, axis), axis=0)  15.4 us
    another operation x29, local copies, waits for them, and re-layouts, local(): jax.scipy.linalg.solve_triangular(diag_block, current[offset:offset + PAN...  15.2 us
    dot_general x4, matrix products, local(): update = jnp.dot(panel_cols, solved, preferred_element_type=jnp.float32)  13 us
  transfers between devices with their start and end apart: 7, of which 4 were waited for; matrix products, arithmetic and copies ran while one was open for 21% of the time, Pallas kernels for 0%

profile of v1, /device:TPU:0, one launch (start us, length us, event | category | flops | bytes accessed | tf_op | source)
XLA Modules:
  0.0 357.5 jit_solution(5562600036931569421)
XLA Ops:
  7.2 0.7 all-gather.14.cloned.1.call-update
  8.0 0.7 select_reduce_fusion
  8.7 3.5 convert_select_fusion
  12.2 80.8 %all-gather.14.cloned.1.call-done = bf16[1,2048,1024]{2,1,0:T(8,128)(2,1)} async-done(((bf16[1,512,1024]{2,1,0:T(8,128)(2,1)}), bf16[1,2048,1024]{2,1,0:T(8,128)(2,1)}) %all-gather.14.cloned.1.call-update) | async-done | bytes 4194320 | tf_op jit(solution)/shard_map/all_gather | solution.py:50
  93.0 1.2 fusion.16
  94.3 4.0 %while.12 = (s32[]{:T(128)}, f32[256,256]{1,0:T(8,128)S(1)}, s32[2,2]{1,0:T(2,128)S(1)}, f32[2,128,128]{2,1,0:T(8,128)S(1)}, s32[]{:T(128)}) while((s32[]{:T(128)}, f32[256,256]{1,0:T(8,128)S(1)}, s32[2,2]{1,0:T(2,128)S(1)}, f32[2,128,128]{2,1,0:T(8,128)S(1)}, s32[]{:T(128)}) %tuple.87), condition=%wide.while_cond.4, body=%wide.while_body.4.sunk | while | flops 2 | bytes 131181 | solution.py:57
  94.9 1.4 bitcast_dynamic-update-slice_fusion.8
  96.9 1.4 bitcast_dynamic-update-slice_fusion.8
  98.3 19.7 %custom-call.6 = f32[2,128,128]{1,2,0:T(8,128)S(1)} custom-call(f32[2,128,128]{2,1,0:T(8,128)S(1)} %get-tuple-element.77), custom_call_target="InvertDiagBlocksLowerTriangular" | custom-call | tf_op jit(solution)/shard_map/jit(_solve_triangular)/triangular_solve | solution.py:57
  118.0 1.4 fusion.26
  119.4 1.3 convolution_subtract_fusion.3
  121.1 0.7 fusion.12
  122.0 3.8 %while.13 = (s32[]{:T(128)}, f32[256,256]{1,0:T(8,128)S(1)}, s32[2,2]{1,0:T(2,128)S(1)}, f32[2,128,128]{2,1,0:T(8,128)S(1)}, s32[]{:T(128)}) while((s32[]{:T(128)}, f32[256,256]{1,0:T(8,128)S(1)}, s32[2,2]{1,0:T(2,128)S(1)}, f32[2,128,128]{2,1,0:T(8,128)S(1)}, s32[]{:T(128)}) %tuple.113), condition=%wide.while_cond.4.clone, body=%wide.while_body.4.clone.sunk | while | flops 2 | bytes 131181 | solution.py:57
  122.6 1.3 bitcast_dynamic-update-slice_fusion.9
  124.5 1.3 bitcast_dynamic-update-slice_fusion.9
  125.7 19.7 %custom-call.7 = f32[2,128,128]{1,2,0:T(8,128)S(1)} custom-call(f32[2,128,128]{2,1,0:T(8,128)S(1)} %get-tuple-element.78), custom_call_target="InvertDiagBlocksLowerTriangular" | custom-call | tf_op jit(solution)/shard_map/jit(_solve_triangular)/triangular_solve | solution.py:57
  145.5 1.5 reduce_sum.58
  146.9 3.3 subtract_select_fusion.3
  150.8 1.5 copy-done.2
  153.1 0.7 fusion.11
  154.2 3.8 %while.14 = (s32[]{:T(128)}, f32[256,256]{1,0:T(8,128)S(1)}, s32[2,2]{1,0:T(2,128)S(1)}, f32[2,128,128]{2,1,0:T(8,128)S(1)}, s32[]{:T(128)}) while((s32[]{:T(128)}, f32[256,256]{1,0:T(8,128)S(1)}, s32[2,2]{1,0:T(2,128)S(1)}, f32[2,128,128]{2,1,0:T(8,128)S(1)}, s32[]{:T(128)}) %tuple.114), condition=%wide.while_cond.4.clone.1, body=%wide.while_body.4.clone.1.sunk | while | flops 2 | bytes 131181 | solution.py:57
  154.8 1.3 bitcast_dynamic-update-slice_fusion.10
  156.1 0.6 fusion.74
  156.7 1.3 bitcast_dynamic-update-slice_fusion.10
  158.0 19.7 %custom-call.8 = f32[2,128,128]{1,2,0:T(8,128)S(1)} custom-call(f32[2,128,128]{2,1,0:T(8,128)S(1)} %get-tuple-element.79), custom_call_target="InvertDiagBlocksLowerTriangular" | custom-call | tf_op jit(solution)/shard_map/jit(_solve_triangular)/triangular_solve | solution.py:57
  177.7 1.5 reduce_sum.59
  179.1 3.2 subtract_select_fusion.2
  183.0 1.5 copy-done.1
  185.3 0.7 fusion.10
  186.1 3.8 %while.15 = (s32[]{:T(128)}, f32[256,256]{1,0:T(8,128)S(1)}, s32[2,2]{1,0:T(2,128)S(1)}, f32[2,128,128]{2,1,0:T(8,128)S(1)}, s32[]{:T(128)}) while((s32[]{:T(128)}, f32[256,256]{1,0:T(8,128)S(1)}, s32[2,2]{1,0:T(2,128)S(1)}, f32[2,128,128]{2,1,0:T(8,128)S(1)}, s32[]{:T(128)}) %tuple.115), condition=%wide.while_cond.4.clone.2, body=%wide.while_body.4.clone.2.sunk | while | flops 2 | bytes 131181 | solution.py:57
  186.8 1.3 bitcast_dynamic-update-slice_fusion.11
  188.7 1.3 bitcast_dynamic-update-slice_fusion.11
  189.9 19.7 %custom-call.9 = f32[2,128,128]{1,2,0:T(8,128)S(1)} custom-call(f32[2,128,128]{2,1,0:T(8,128)S(1)} %get-tuple-element.80), custom_call_target="InvertDiagBlocksLowerTriangular" | custom-call | tf_op jit(solution)/shard_map/jit(_solve_triangular)/triangular_solve | solution.py:57
  209.7 1.5 reduce_sum.60
  211.1 3.2 subtract_select_fusion.1
  214.9 1.5 copy-done
  217.3 0.7 fusion.9
  218.1 15.3 %all-gather.22.cloned.1.call-done = bf16[1024,512]{1,0:T(8,128)(2,1)} async-done(((bf16[256,512]{1,0:T(8,128)(2,1)}), bf16[1024,512]{1,0:T(8,128)(2,1)}) %all-gather.22.cloned.1.call-update) | async-done | bytes 1048592 | tf_op jit(solution)/shard_map/all_gather | solution.py:14
  233.4 1.5 reduce_sum.61
  234.9 3.2 subtract_select_fusion
  238.1 1.6 fusion.19
  240.0 27.9 %all-gather.12.cloned.1.call-done = bf16[256,2048]{1,0:T(8,128)(2,1)} async-done(((bf16[256,512]{1,0:T(8,128)(2,1)}), bf16[256,2048]{1,0:T(8,128)(2,1)}) %all-gather.12.cloned.1.call-update) | async-done | bytes 1048592 | tf_op jit(solution)/shard_map/all_gather | solution.py:71
  267.9 1.5 copy.19
  269.4 0.8 convolution_convert_fusion.1
  270.2 0.9 copy.20
  271.2 5.6 %convolution_convert_fusion = bf16[4096,1024]{1,0:T(8,128)(2,1)} fusion(bf16[256,4096]{1,0:T(8,128)(2,1)S(1)} %bitcast.109, s32[]{:T(128)S(6)} %select_n.126), kind=kOutput, calls=%fused_computation.8 | convolution fusion | flops 2151677952 | bytes 11010052 | tf_op jit(solution)/shard_map/dot_general | solution.py:75
  276.8 71.0 %reduce-scatter.2.cloned.1.call-done = bf16[512,1024]{1,0:T(8,128)(2,1)} async-done(((bf16[4096,1024]{1,0:T(8,128)(2,1)}), bf16[512,1024]{1,0:T(8,128)(2,1)}) %reduce-scatter.2.cloned.1.call-update) | async-done | bytes 1048592 | tf_op jit(solution)/shard_map/reduce_scatter | solution.py:74
  347.9 2.8 convert_subtract_fusion
  (67 shorter events, 9.6 us)
Async XLA Ops:
  7.2 85.9 %all-gather.14.cloned.1.call-start = ((), (), s32[]{:S(2)}) async-start(), calls=%async_computation.3 | async-start | bytes 5242880 | tf_op jit(solution)/shard_map/all_gather | solution.py:50
  7.9 137.6 %all-gather.16.cloned.1.call-start = ((), (), s32[]{:S(2)}) async-start(), calls=%async_computation.4 | async-start | bytes 1310720 | tf_op jit(solution)/shard_map/all_gather | solution.py:14
  12.2 134.7 %copy-start.4 = (bf16[1,2048,512]{2,1,0:T(8,128)(2,1)S(1)}, bf16[1,2048,512]{2,1,0:T(8,128)(2,1)}, u32[]{:S(2)}) copy-start(bf16[1,2048,512]{2,1,0:T(8,128)(2,1)} %param.16) | copy-start | bytes 6291460
  121.9 55.8 %all-gather.18.cloned.1.call-start = ((), (), s32[]{:S(2)}) async-start(), calls=%async_computation.5 | async-start | bytes 1310720 | tf_op jit(solution)/shard_map/all_gather | solution.py:14
  150.3 2.0 copy-start.2
  153.9 55.8 %all-gather.20.cloned.1.call-start = ((), (), s32[]{:S(2)}) async-start(), calls=%async_computation.6 | async-start | bytes 1310720 | tf_op jit(solution)/shard_map/all_gather | solution.py:14
  182.5 2.0 copy-start.1
  186.1 47.3 %all-gather.22.cloned.1.call-start = ((), (), s32[]{:S(2)}) async-start(), calls=%async_computation.7 | async-start | bytes 1310720 | tf_op jit(solution)/shard_map/all_gather | solution.py:14
  214.5 2.0 copy-start
  218.0 49.8 %all-gather.12.cloned.1.call-start = ((), (), s32[]{:S(2)}) async-start(), calls=%async_computation.1 | async-start | bytes 1310720 | tf_op jit(solution)/shard_map/all_gather | solution.py:71
  234.9 34.5 %copy-start.6 = (s32[1,8]{1,0:T(1,128)S(1)}, s32[1,8]{1,0:T(1,128)}, u32[]{:S(2)}) copy-start(s32[1,8]{1,0:T(1,128)} %param.18) | copy-start | bytes 100
  239.7 31.5 %copy-start.3 = (bf16[2048,512]{1,0:T(8,128)(2,1)}, bf16[2048,512]{1,0:T(8,128)(2,1)S(1)}, u32[]{:S(2)}) copy-start(bf16[2048,512]{1,0:T(8,128)(2,1)S(1)} %get-tuple-element.126) | copy-start | bytes 6291460
  239.7 108.1 %reduce-scatter.2.cloned.1.call-start = ((), (), s32[]{:S(2)}) async-start(), calls=%async_computation.2 | async-start | bytes 9437184 | tf_op jit(solution)/shard_map/reduce_scatter | solution.py:74
  276.8 71.1 %copy-start.5 = (f32[512,1024]{1,0:T(8,128)S(1)}, f32[512,1024]{1,0:T(8,128)}, u32[]{:S(2)}) copy-start(f32[512,1024]{1,0:T(8,128)} %param.19) | copy-start | bytes 6291460
Sparse Core Ops, SparseCore 0:
  9.5 83.4 all-gather.13
  122.0 15.3 all-gather.15
  154.0 15.5 all-gather.17
  186.2 15.3 all-gather.19
  218.2 15.1 all-gather.21
  239.8 27.9 all-gather.11
  276.9 70.8 reduce-scatter.1
